TPU v7x, 256 devices: a whole 4x4x8 slice. The times are simulated.
256 devices in a mesh: tm: 64 (over z, x, core), blk: 4 (over y).
Axes of the slice: x: 4, y: 4, z: 8, core: 2. Of those that a mesh axis runs over, the one named last changes fastest.
Arguments:
- prior_mean: float32 [512], replicated, may hold values from -6 to 6
- after_mean: float32 [512], replicated, may hold values from -6 to 6
- filter_map: float32 [128, 512, 512], P('tm', 'blk'), may hold values from -1 to 1.5
- smoother_gain: float32 [128, 512, 512], P('tm', 'blk'), may hold values from -1 to 1.5
- smoother_map: float32 [128, 512, 512], P('tm', 'blk'), may hold values from -1 to 1.5
- obs_gain: float32 [128, 512, 128], P('tm', 'blk'), may hold values from -0.5 to 0.5
- observations: float32 [128, 128], P('tm'), may hold values from -6 to 6
Outputs:
- filtered: float32 [128, 512], P('tm', 'blk')
- smoothed: float32 [128, 512], P('tm', 'blk')
All inputs are finite; a program needn't handle non-finite values.
Results may differ from a plain program's by a relative error of at most 0.0003.
Values sent between devices are 32-bit elements; how exact they have to be, the bound alone decides.
A program may use at most 128 MiB of HBM per device.

v0:
```python
import jax
import jax.numpy as jnp
from jax import lax
from jax.sharding import Mesh
from jax.sharding import PartitionSpec as P

TM = ("tm_0", "tm_1", "tm_2")


def neutral_like(value, identity):
    return jax.tree.map(
        lambda part, zero: jnp.zeros_like(part) + jnp.asarray(zero, part.dtype), value, identity
    )


def prefix_by_axis(value, axes, combine, identity, reverse):
    before = start = neutral_like(value, identity)
    so_far = value
    for axis in reversed(axes):
        length, index = (lax.axis_size(axis), lax.axis_index(axis))
        pieces = jax.tree.map(lambda part: lax.all_gather(part, axis), so_far)
        inside, so_far = (start, start)
        for k in reversed(range(length)) if reverse else range(length):
            passed = k > index if reverse else k < index
            so_far = combine(so_far, jax.tree.map(lambda part: part[k], pieces))
            inside = jax.tree.map(lambda new, old: jnp.where(passed, new, old), so_far, inside)
        before = combine(inside, before)
    return before


def chain_combine(earlier, later):
    highest = lax.Precision.HIGHEST
    joined_map = jnp.dot(later[0], earlier[0], precision=highest)
    joined_offset = jnp.dot(later[0], earlier[1], precision=highest) + later[1]
    return (joined_map, joined_offset)


def shards(prior_mean, after_mean, filter_map, smoother_gain, smoother_map, obs_gain, observations):
    highest = lax.Precision.HIGHEST
    steps = filter_map.shape[0]
    rows = filter_map.shape[1]
    width = filter_map.shape[2]
    first_row = lax.axis_index("blk") * rows
    drive_rows = jnp.einsum("tro,to->tr", obs_gain, observations, precision=highest)
    full_filter, full_gain, drive = (
        lax.all_gather(filter_map, "blk", axis=1, tiled=True),
        lax.all_gather(smoother_gain, "blk", axis=1, tiled=True),
        lax.all_gather(drive_rows, "blk", axis=1, tiled=True),
    )
    identity = jnp.eye(width, dtype=jnp.float32)
    nothing = jnp.zeros((width,), jnp.float32)
    offset = nothing
    for index in range(steps):
        offset = jnp.dot(full_filter[index], offset, precision=highest) + drive[index]
    composite = full_filter[steps - 1]
    index = 0
    composite = jnp.dot(composite, full_filter[index], precision=highest)
    total = prefix_by_axis((composite, offset), TM, chain_combine, (identity, nothing), False)
    entering = jnp.dot(total[0], prior_mean, precision=highest) + total[1]
    current = entering
    filtered_list = []
    for index in range(steps):
        current = jnp.dot(full_filter[index], current, precision=highest) + drive[index]
        filtered_list.append(current)
    filtered_full = jnp.stack(filtered_list, axis=0)
    filtered_rows = lax.dynamic_slice_in_dim(filtered_full, first_row, rows, 1)
    pulled_rows = jnp.einsum("trk,tk->tr", smoother_map, filtered_full, precision=highest)
    pulled = lax.all_gather(pulled_rows, "blk", axis=1, tiled=True)
    offset = nothing
    for index in range(steps - 1, -1, -1):
        offset = jnp.dot(full_gain[index], offset, precision=highest) + pulled[index]
    composite = full_gain[0]
    index = 1
    composite = jnp.dot(composite, full_gain[index], precision=highest)
    total = prefix_by_axis((composite, offset), TM, chain_combine, (identity, nothing), True)
    leaving = jnp.dot(total[0], after_mean, precision=highest) + total[1]
    current = leaving
    smoothed_list = []
    for index in range(steps - 1, -1, -1):
        current = jnp.dot(full_gain[index], current, precision=highest) + pulled[index]
        smoothed_list.append(current)
    smoothed_full = jnp.stack(smoothed_list[::-1], axis=0)
    smoothed_rows = lax.dynamic_slice_in_dim(smoothed_full, first_row, rows, 1)
    return (filtered_rows, smoothed_rows)


def solution(mesh):
    torus = Mesh(mesh.devices.reshape(8, 4, 2, mesh.shape["blk"]), ("tm_0", "tm_1", "tm_2", "blk"))
    in_specs = (
        P(),
        P(),
        P(TM, "blk", None),
        P(TM, "blk", None),
        P(TM, "blk", None),
        P(TM, "blk", None),
        P(TM, None),
    )
    out_specs = (P(TM, "blk"), P(TM, "blk"))
    return jax.shard_map(
        shards, mesh=torus, in_specs=in_specs, out_specs=out_specs, check_vma=False
    )
```

profile of v0, /device:TPU:1, one launch (start us, length us, event | category | flops | bytes accessed | tf_op | source)
XLA Modules:
  0.0 462.8 jit_solution(7283257458123513231)
XLA Ops:
  8.7 38.1 %all-gather.27.cloned.1.call-done = f32[2,512,512]{2,1,0:T(8,128)} async-done(((f32[2,128,512]{2,1,0:T(8,128)}), f32[2,512,512]{2,1,0:T(8,128)}) %all-gather.27.cloned.1.call-update) | async-done | bytes 2097168 | tf_op jit(solution)/shard_map/all_gather | solution.py:46
  46.8 4.4 fusion.142
  51.2 30.8 %all-gather.29.cloned.1.call-done = f32[2,512,512]{2,1,0:T(8,128)} async-done(((f32[2,128,512]{2,1,0:T(8,128)}), f32[2,512,512]{2,1,0:T(8,128)}) %all-gather.29.cloned.1.call-update) | async-done | bytes 2097168 | tf_op jit(solution)/shard_map/all_gather | solution.py:47
  82.0 4.4 fusion.147
  86.5 14.2 %all-gather.31.cloned.1.call-done = f32[1024,512]{1,0:T(8,128)} async-done(((f32[512,512]{1,0:T(8,128)}), f32[1024,512]{1,0:T(8,128)}) %all-gather.31.cloned.1.call-update) | async-done | bytes 2097168 | tf_op jit(solution)/shard_map/all_gather | solution.py:21
  102.9 4.4 fusion.136
  107.4 12.2 %all-gather.37.cloned.1.call-done = f32[1024,512]{1,0:T(8,128)} async-done(((f32[512,512]{1,0:T(8,128)}), f32[1024,512]{1,0:T(8,128)}) %all-gather.37.cloned.1.call-update) | async-done | bytes 2097168 | tf_op jit(solution)/shard_map/all_gather | solution.py:21
  121.8 4.4 fusion.84
  126.4 46.0 %all-gather.33.cloned.1.call-done = f32[2048,512]{1,0:T(8,128)} async-done(((f32[512,512]{1,0:T(8,128)}), f32[2048,512]{1,0:T(8,128)}) %all-gather.33.cloned.1.call-update) | async-done | bytes 4194320 | tf_op jit(solution)/shard_map/all_gather | solution.py:21
  175.8 3.1 fusion.121
  182.7 2.8 fusion.129
  186.0 8.1 %all_gather.91 = f32[2,512]{1,0:T(2,128)S(1)} all-gather(f32[2,128]{1,0:T(2,128)S(1)} %bitcast.347), channel_id=1, replica_groups=mesh['tm_0'=8,'tm_1'=4,'tm_2'=2,'blk'=4] {'blk'}, dimensions={1}, use_global_device_ids=true | all-gather | bytes 5120 | tf_op jit(solution)/shard_map/all_gather | solution.py:48
  198.5 4.2 all-gather.12
  203.6 21.6 %all-gather.39.cloned.1.call-done = f32[2048,512]{1,0:T(8,128)} async-done(((f32[512,512]{1,0:T(8,128)}), f32[2048,512]{1,0:T(8,128)}) %all-gather.39.cloned.1.call-update) | async-done | bytes 4194320 | tf_op jit(solution)/shard_map/all_gather | solution.py:21
  228.5 3.1 fusion.69
  235.5 2.8 fusion.77
  238.4 2.5 fusion.134
  243.2 9.4 %all-gather.13 = f32[4,1,512]{2,1,0:T(1,128)S(1)} all-gather(f32[1,1,512]{2,1,0:T(1,128)S(1)} %bitcast.331), channel_id=6, replica_groups=mesh['tm_0'=8,'tm_1'=4,'tm_2'=2,'blk'=4] {'tm_1'}, dimensions={0}, use_global_device_ids=true | all-gather | bytes 10240 | tf_op jit(solution)/shard_map/all_gather | solution.py:21
  261.7 22.3 %all-gather.14 = f32[8,1,512]{2,1,0:T(1,128)S(1)} all-gather(f32[1,1,512]{2,1,0:T(1,128)S(1)} %bitcast.342), channel_id=7, replica_groups=mesh['tm_0'=8,'tm_1'=4,'tm_2'=2,'blk'=4] {'tm_0'}, dimensions={0}, use_global_device_ids=true | all-gather | bytes 18432 | tf_op jit(solution)/shard_map/all_gather | solution.py:21
  284.0 2.4 fusion.67
  287.4 3.0 fusion.6
  290.4 3.0 fusion.20
  293.4 28.4 %all-gather.35.cloned.1.call-done = f32[4096,512]{1,0:T(8,128)} async-done(((f32[512,512]{1,0:T(8,128)}), f32[4096,512]{1,0:T(8,128)}) %all-gather.35.cloned.1.call-update) | async-done | bytes 8388624 | tf_op jit(solution)/shard_map/all_gather | solution.py:21
  324.1 2.3 fusion.93
  326.5 2.5 fusion.97
  361.3 8.5 %all_gather.105 = f32[2,512]{1,0:T(2,128)S(1)} all-gather(f32[2,128]{1,0:T(2,128)S(1)} %bitcast.346), channel_id=1, replica_groups=mesh['tm_0'=8,'tm_1'=4,'tm_2'=2,'blk'=4] {'blk'}, dimensions={1}, use_global_device_ids=true | all-gather | bytes 5120 | tf_op jit(solution)/shard_map/all_gather | solution.py:68
  370.8 3.6 all-gather.15
  375.4 9.5 %all-gather.16 = f32[4,1,512]{2,1,0:T(1,128)S(1)} all-gather(f32[1,1,512]{2,1,0:T(1,128)S(1)} %bitcast.330), channel_id=12, replica_groups=mesh['tm_0'=8,'tm_1'=4,'tm_2'=2,'blk'=4] {'tm_1'}, dimensions={0}, use_global_device_ids=true | all-gather | bytes 10240 | tf_op jit(solution)/shard_map/all_gather | solution.py:21
  387.9 19.5 %all-gather.17 = f32[8,1,512]{2,1,0:T(1,128)S(1)} all-gather(f32[1,1,512]{2,1,0:T(1,128)S(1)} %bitcast.339), channel_id=13, replica_groups=mesh['tm_0'=8,'tm_1'=4,'tm_2'=2,'blk'=4] {'tm_0'}, dimensions={0}, use_global_device_ids=true | all-gather | bytes 18432 | tf_op jit(solution)/shard_map/all_gather | solution.py:21
  408.7 7.8 %all-gather.41.cloned.1.call-done = f32[4096,512]{1,0:T(8,128)} async-done(((f32[512,512]{1,0:T(8,128)}), f32[4096,512]{1,0:T(8,128)}) %all-gather.41.cloned.1.call-update) | async-done | bytes 8388624 | tf_op jit(solution)/shard_map/all_gather | solution.py:21
  418.8 2.3 fusion.41
  421.2 2.5 fusion.45
  (206 shorter events, 113.7 us)
Async XLA Ops:
  7.2 353.7 %copy-start = (f32[2,128,512]{2,1,0:T(8,128)S(1)}, f32[2,128,512]{2,1,0:T(8,128)}, u32[]{:S(2)}) copy-start(f32[2,128,512]{2,1,0:T(8,128)} %param.11) | copy-start | bytes 1572868
  7.2 39.6 %all-gather.27.cloned.1.call-start = ((), (), s32[]{:S(2)}) async-start(), calls=%async_computation | async-start | bytes 2621440 | tf_op jit(solution)/shard_map/all_gather | solution.py:46
  7.9 74.1 %all-gather.29.cloned.1.call-start = ((), (), s32[]{:S(2)}) async-start(), calls=%async_computation.1 | async-start | bytes 2621440 | tf_op jit(solution)/shard_map/all_gather | solution.py:47
  8.7 92.0 %all-gather.31.cloned.1.call-start = ((), (), s32[]{:S(2)}) async-start(), calls=%async_computation.2 | async-start | bytes 3145728 | tf_op jit(solution)/shard_map/all_gather | solution.py:21
  51.2 68.4 %all-gather.37.cloned.1.call-start = ((), (), s32[]{:S(2)}) async-start(), calls=%async_computation.5 | async-start | bytes 3145728 | tf_op jit(solution)/shard_map/all_gather | solution.py:21
  86.4 86.0 %all-gather.33.cloned.1.call-start = ((), (), s32[]{:S(2)}) async-start(), calls=%async_computation.3 | async-start | bytes 5242880 | tf_op jit(solution)/shard_map/all_gather | solution.py:21
  102.9 23.3 %copy-start.13 = (f32[512,512]{1,0:T(8,128)}, f32[512,512]{1,0:T(8,128)S(1)}, u32[]{:S(2)}) copy-start(f32[512,512]{1,0:T(8,128)S(1)} %fusion.35) | copy-start | bytes 3145732
  107.3 117.9 %all-gather.39.cloned.1.call-start = ((), (), s32[]{:S(2)}) async-start(), calls=%async_computation.6 | async-start | bytes 5242880 | tf_op jit(solution)/shard_map/all_gather | solution.py:21
  121.8 53.0 %copy-start.16 = (f32[512,512]{1,0:T(8,128)}, f32[512,512]{1,0:T(8,128)S(1)}, u32[]{:S(2)}) copy-start(f32[512,512]{1,0:T(8,128)S(1)} %fusion.31) | copy-start | bytes 3145732
  126.2 195.6 %all-gather.35.cloned.1.call-start = ((), (), s32[]{:S(2)}) async-start(), calls=%async_computation.4 | async-start | bytes 9437184 | tf_op jit(solution)/shard_map/all_gather | solution.py:21
  172.4 7.4 %copy-start.7 = (f32[2048,512]{1,0:T(8,128)S(1)}, f32[2048,512]{1,0:T(8,128)}, u32[]{:S(2)}) copy-start(f32[2048,512]{1,0:T(8,128)} %all-gather.33.cloned.1.call-done) | copy-start | bytes 12582916
  179.8 22.9 %copy-start.3 = (f32[2,512,512]{2,1,0:T(8,128)S(1)}, f32[2,512,512]{2,1,0:T(8,128)}, u32[]{:S(2)}) copy-start(f32[2,512,512]{2,1,0:T(8,128)} %all-gather.29.cloned.1.call-done) | copy-start | bytes 6291460
  185.6 231.0 %all-gather.41.cloned.1.call-start = ((), (), s32[]{:S(2)}) async-start(), calls=%async_computation.7 | async-start | bytes 9437184 | tf_op jit(solution)/shard_map/all_gather | solution.py:21
  225.2 7.4 %copy-start.5 = (f32[2048,512]{1,0:T(8,128)S(1)}, f32[2048,512]{1,0:T(8,128)}, u32[]{:S(2)}) copy-start(f32[2048,512]{1,0:T(8,128)} %all-gather.39.cloned.1.call-done) | copy-start | bytes 12582916
  238.3 16.9 %copy-start.14 = (f32[512,512]{1,0:T(8,128)S(1)}, f32[512,512]{1,0:T(8,128)}, u32[]{:S(2)}) copy-start(f32[512,512]{1,0:T(8,128)} %copy-done.13) | copy-start | bytes 3145732
  238.3 16.9 %copy-start.15 = (f32[512,512]{1,0:T(8,128)S(1)}, f32[512,512]{1,0:T(8,128)}, u32[]{:S(2)}) copy-start(f32[512,512]{1,0:T(8,128)} %fusion.136) | copy-start | bytes 3145732
  238.3 18.1 %copy-start.17 = (f32[512,512]{1,0:T(8,128)S(1)}, f32[512,512]{1,0:T(8,128)}, u32[]{:S(2)}) copy-start(f32[512,512]{1,0:T(8,128)} %copy-done.16) | copy-start | bytes 3145732
  238.3 18.1 %copy-start.18 = (f32[512,512]{1,0:T(8,128)S(1)}, f32[512,512]{1,0:T(8,128)}, u32[]{:S(2)}) copy-start(f32[512,512]{1,0:T(8,128)} %fusion.84) | copy-start | bytes 3145732
  240.8 16.8 %copy-start.8 = (f32[2048,512]{1,0:T(8,128)S(1)}, f32[2048,512]{1,0:T(8,128)}, u32[]{:S(2)}) copy-start(f32[2048,512]{1,0:T(8,128)} %all-gather.33.cloned.1.call-done) | copy-start | bytes 12582916
  256.4 31.0 %copy-start.10 = (f32[512,512]{1,0:T(8,128)S(1)}, f32[512,512]{1,0:T(8,128)}, u32[]{:S(2)}) copy-start(f32[512,512]{1,0:T(8,128)} %copy-done.9) | copy-start | bytes 3145732
  256.4 31.0 %copy-start.12 = (f32[512,512]{1,0:T(8,128)S(1)}, f32[512,512]{1,0:T(8,128)}, u32[]{:S(2)}) copy-start(f32[512,512]{1,0:T(8,128)} %copy-done.11) | copy-start | bytes 3145732
  256.4 31.0 %copy-start.25 = (f32[512,512]{1,0:T(8,128)S(1)}, f32[512,512]{1,0:T(8,128)}, u32[]{:S(2)}) copy-start(f32[512,512]{1,0:T(8,128)} %fusion.129) | copy-start | bytes 3145732
  256.4 31.0 %copy-start.27 = (f32[512,512]{1,0:T(8,128)S(1)}, f32[512,512]{1,0:T(8,128)}, u32[]{:S(2)}) copy-start(f32[512,512]{1,0:T(8,128)} %copy-done.26) | copy-start | bytes 3145732
  257.6 32.8 %copy-start.31 = (f32[512,512]{1,0:T(8,128)}, f32[512,512]{1,0:T(8,128)S(1)}, u32[]{:S(2)}) copy-start(f32[512,512]{1,0:T(8,128)S(1)} %fusion.15) | copy-start | bytes 3145732
  284.0 6.4 %copy-start.22 = (f32[512,512]{1,0:T(8,128)S(1)}, f32[512,512]{1,0:T(8,128)}, u32[]{:S(2)}) copy-start(f32[512,512]{1,0:T(8,128)} %copy-done.21) | copy-start | bytes 3145732
  321.8 18.5 %copy-start.30 = (f32[512,512]{1,0:T(8,128)S(1)}, f32[512,512]{1,0:T(8,128)}, u32[]{:S(2)}) copy-start(f32[512,512]{1,0:T(8,128)} %fusion.6) | copy-start | bytes 3145732
  324.1 17.1 %copy-start.2 = (f32[4096,512]{1,0:T(8,128)S(1)}, f32[4096,512]{1,0:T(8,128)}, u32[]{:S(2)}) copy-start(f32[4096,512]{1,0:T(8,128)} %all-gather.35.cloned.1.call-done) | copy-start | bytes 25165828
  353.6 20.8 %copy-start.33 = (f32[1024,512]{1,0:T(8,128)S(1)}, f32[1024,512]{1,0:T(8,128)}, u32[]{:S(2)}) copy-start(f32[1024,512]{1,0:T(8,128)} %all-gather.37.cloned.1.call-done) | copy-start | bytes 6291460
  355.9 28.9 %copy-start.6 = (f32[2048,512]{1,0:T(8,128)S(1)}, f32[2048,512]{1,0:T(8,128)}, u32[]{:S(2)}) copy-start(f32[2048,512]{1,0:T(8,128)} %all-gather.39.cloned.1.call-done) | copy-start | bytes 12582916
  358.8 48.9 %copy-start.32 = (f32[512,512]{1,0:T(8,128)S(1)}, f32[512,512]{1,0:T(8,128)}, u32[]{:S(2)}) copy-start(f32[512,512]{1,0:T(8,128)} %copy-done.31) | copy-start | bytes 3145732
  416.5 18.3 %copy-start.24 = (f32[512,512]{1,0:T(8,128)S(1)}, f32[512,512]{1,0:T(8,128)}, u32[]{:S(2)}) copy-start(f32[512,512]{1,0:T(8,128)} %fusion.20) | copy-start | bytes 3145732
  418.8 17.0 %copy-start.1 = (f32[4096,512]{1,0:T(8,128)S(1)}, f32[4096,512]{1,0:T(8,128)}, u32[]{:S(2)}) copy-start(f32[4096,512]{1,0:T(8,128)} %all-gather.41.cloned.1.call-done) | copy-start | bytes 25165828
  (14 other events, 48.1 us)
Sparse Core Ops, SparseCore 0:
  9.8 36.9 all-gather.26
  48.6 33.3 all-gather.28
  83.8 16.8 all-gather.30
  102.3 17.1 all-gather.36
  121.2 51.1 all-gather.32
  174.1 51.0 all-gather.38
  227.0 94.7 all-gather.34
  323.6 92.9 all-gather.40
where the time goes:
time: 471 us; the launch traced here: 463 us
  waiting for transfers between devices  200 us (42%)
  matrix products  155 us (33%)
  blocking collectives  85.1 us (18%)
  between operations  15.1 us (3%)
  local copies, waits for them, and re-layouts  6.15 us (1%)
    all_gather x6, waiting for transfers between devices, prefix_by_axis(): pieces = jax.tree.map(lambda part: lax.all_gather(part, axis), so_far)  130 us
    dot_general x34, matrix products, chain_combine(): joined_map = jnp.dot(later[0], earlier[0], precision=highest)  74.4 us
    all_gather x6, blocking collectives, prefix_by_axis(): pieces = jax.tree.map(lambda part: lax.all_gather(part, axis), so_far)  68.5 us
    dot_general x34, matrix products, chain_combine(): joined_offset = jnp.dot(later[0], earlier[1], precision=highest) + later[1]  58.5 us
    all_gather x1, waiting for transfers between devices, shards(): lax.all_gather(filter_map, 'blk', axis=1, tiled=True)  38.1 us
    all_gather x1, waiting for transfers between devices, shards(): lax.all_gather(smoother_gain, 'blk', axis=1, tiled=True)  30.8 us
  transfers between devices with their start and end apart: 8, of which 8 were waited for; matrix products, arithmetic and copies ran while one was open for 25% of the time, Pallas kernels for 0%

commit v1 on v0

--- a/solution.py
+++ b/solution.py
@@ -43,7 +43,7 @@
     first_row = lax.axis_index("blk") * rows
     drive_rows = jnp.einsum("tro,to->tr", obs_gain, observations, precision=highest)
     full_filter, full_gain, drive = (
-        lax.all_gather(filter_map, "blk", axis=1, tiled=True),
+        jnp.concatenate(lax.all_gather(filter_map, "blk"), axis=1),
         lax.all_gather(smoother_gain, "blk", axis=1, tiled=True),
         lax.all_gather(drive_rows, "blk", axis=1, tiled=True),
     )

time: 471 us -> 473 us (level)
  waiting for transfers between devices: 200 us -> 192 us
  matrix products: 155 us -> 160 us
    all_gather x6, waiting for transfers between devices: 130 us -> 122 us  [prefix_by_axis(): pieces = jax.tree.map(lambda part: lax.all_gather(part, axis), so_far)]
    dot_general x34, matrix products: 74.4 us -> 79.5 us  [chain_combine(): joined_map = jnp.dot(later[0], earlier[0], precision=highest)]
  transfers between devices with their start and end apart: 8 -> 8, of which waited for: 8 -> 8; matrix products, arithmetic and copies ran while one was open for 25% -> 26% of each run, Pallas kernels for 0% -> 0%
where the time goes in v1:
time: 473 us; the launch traced here: 464 us
  waiting for transfers between devices  192 us (41%)
  matrix products  160 us (34%)
  blocking collectives  85 us (18%)
  between operations  15.1 us (3%)
  local copies, waits for them, and re-layouts  9.85 us (2%)
    all_gather x6, waiting for transfers between devices, prefix_by_axis(): pieces = jax.tree.map(lambda part: lax.all_gather(part, axis), so_far)  122 us
    dot_general x34, matrix products, chain_combine(): joined_map = jnp.dot(later[0], earlier[0], precision=highest)  79.5 us
    all_gather x6, blocking collectives, prefix_by_axis(): pieces = jax.tree.map(lambda part: lax.all_gather(part, axis), so_far)  68 us
    dot_general x34, matrix products, chain_combine(): joined_offset = jnp.dot(later[0], earlier[1], precision=highest) + later[1]  60.7 us
    all_gather x1, waiting for transfers between devices, shards(): lax.all_gather(filter_map, 'blk')  38.1 us
    all_gather x1, waiting for transfers between devices, shards(): lax.all_gather(smoother_gain, 'blk', axis=1, tiled=True)  30.6 us
  transfers between devices with their start and end apart: 8, of which 8 were waited for; matrix products, arithmetic and copies ran while one was open for 26% of the time, Pallas kernels for 0%

profile of v1, /device:TPU:1, one launch (start us, length us, event | category | flops | bytes accessed | tf_op | source)
XLA Modules:
  0.0 464.0 jit_solution(11834989300654912959)
XLA Ops:
  8.7 38.1 %all-gather.30.cloned.1.call-done = f32[8,128,512]{2,1,0:T(8,128)} async-done(((f32[2,128,512]{2,1,0:T(8,128)}), f32[8,128,512]{2,1,0:T(8,128)}) %all-gather.30.cloned.1.call-update) | async-done | bytes 2097168 | tf_op jit(solution)/shard_map/all_gather | solution.py:46
  48.5 2.8 fusion.188
  51.4 30.6 %all-gather.28.cloned.1.call-done = f32[2,512,512]{2,1,0:T(8,128)} async-done(((f32[2,128,512]{2,1,0:T(8,128)}), f32[2,512,512]{2,1,0:T(8,128)}) %all-gather.28.cloned.1.call-update) | async-done | bytes 2097168 | tf_op jit(solution)/shard_map/all_gather | solution.py:47
  82.0 4.4 fusion.142
  86.5 14.2 %all-gather.32.cloned.1.call-done = f32[1024,512]{1,0:T(8,128)} async-done(((f32[512,512]{1,0:T(8,128)}), f32[1024,512]{1,0:T(8,128)}) %all-gather.32.cloned.1.call-update) | async-done | bytes 2097168 | tf_op jit(solution)/shard_map/all_gather | solution.py:21
  103.9 4.0 fusion.136
  108.0 11.6 %all-gather.38.cloned.1.call-done = f32[1024,512]{1,0:T(8,128)} async-done(((f32[512,512]{1,0:T(8,128)}), f32[1024,512]{1,0:T(8,128)}) %all-gather.38.cloned.1.call-update) | async-done | bytes 2097168 | tf_op jit(solution)/shard_map/all_gather | solution.py:21
  122.8 4.1 fusion.84
  127.1 45.3 %all-gather.34.cloned.1.call-done = f32[2048,512]{1,0:T(8,128)} async-done(((f32[512,512]{1,0:T(8,128)}), f32[2048,512]{1,0:T(8,128)}) %all-gather.34.cloned.1.call-update) | async-done | bytes 4194320 | tf_op jit(solution)/shard_map/all_gather | solution.py:21
  175.6 3.1 fusion.121
  179.7 3.1 fusion.125
  183.7 4.1 fusion.129
  188.2 8.5 %all_gather.95 = f32[2,512]{1,0:T(2,128)S(1)} all-gather(f32[2,128]{1,0:T(2,128)S(1)} %bitcast.355), channel_id=1, replica_groups=mesh['tm_0'=8,'tm_1'=4,'tm_2'=2,'blk'=4] {'blk'}, dimensions={1}, use_global_device_ids=true | all-gather | bytes 5120 | tf_op jit(solution)/shard_map/all_gather | solution.py:48
  201.1 3.8 all-gather.13
  205.9 19.3 %all-gather.40.cloned.1.call-done = f32[2048,512]{1,0:T(8,128)} async-done(((f32[512,512]{1,0:T(8,128)}), f32[2048,512]{1,0:T(8,128)}) %all-gather.40.cloned.1.call-update) | async-done | bytes 4194320 | tf_op jit(solution)/shard_map/all_gather | solution.py:21
  228.4 3.1 fusion.69
  232.4 3.1 fusion.73
  236.5 4.0 fusion.77
  243.0 2.6 fusion.138
  245.6 9.4 %all-gather.14 = f32[4,1,512]{2,1,0:T(1,128)S(1)} all-gather(f32[1,1,512]{2,1,0:T(1,128)S(1)} %bitcast.339), channel_id=7, replica_groups=mesh['tm_0'=8,'tm_1'=4,'tm_2'=2,'blk'=4] {'tm_1'}, dimensions={0}, use_global_device_ids=true | all-gather | bytes 10240 | tf_op jit(solution)/shard_map/all_gather | solution.py:21
  257.6 2.4 fusion.1
  265.3 22.3 %all-gather.15 = f32[8,1,512]{2,1,0:T(1,128)S(1)} all-gather(f32[1,1,512]{2,1,0:T(1,128)S(1)} %bitcast.350), channel_id=8, replica_groups=mesh['tm_0'=8,'tm_1'=4,'tm_2'=2,'blk'=4] {'tm_0'}, dimensions={0}, use_global_device_ids=true | all-gather | bytes 18432 | tf_op jit(solution)/shard_map/all_gather | solution.py:21
  290.8 3.0 fusion.6
  293.8 3.0 fusion.20
  296.8 25.0 %all-gather.36.cloned.1.call-done = f32[4096,512]{1,0:T(8,128)} async-done(((f32[512,512]{1,0:T(8,128)}), f32[4096,512]{1,0:T(8,128)}) %all-gather.36.cloned.1.call-update) | async-done | bytes 8388624 | tf_op jit(solution)/shard_map/all_gather | solution.py:21
  324.1 2.5 fusion.93
  362.5 8.5 %all_gather.109 = f32[2,512]{1,0:T(2,128)S(1)} all-gather(f32[2,128]{1,0:T(2,128)S(1)} %bitcast.354), channel_id=1, replica_groups=mesh['tm_0'=8,'tm_1'=4,'tm_2'=2,'blk'=4] {'blk'}, dimensions={1}, use_global_device_ids=true | all-gather | bytes 5120 | tf_op jit(solution)/shard_map/all_gather | solution.py:68
  372.0 3.5 all-gather.16
  376.6 9.5 %all-gather.17 = f32[4,1,512]{2,1,0:T(1,128)S(1)} all-gather(f32[1,1,512]{2,1,0:T(1,128)S(1)} %bitcast.338), channel_id=13, replica_groups=mesh['tm_0'=8,'tm_1'=4,'tm_2'=2,'blk'=4] {'tm_1'}, dimensions={0}, use_global_device_ids=true | all-gather | bytes 10240 | tf_op jit(solution)/shard_map/all_gather | solution.py:21
  389.1 19.5 %all-gather.18 = f32[8,1,512]{2,1,0:T(1,128)S(1)} all-gather(f32[1,1,512]{2,1,0:T(1,128)S(1)} %bitcast.347), channel_id=14, replica_groups=mesh['tm_0'=8,'tm_1'=4,'tm_2'=2,'blk'=4] {'tm_0'}, dimensions={0}, use_global_device_ids=true | all-gather | bytes 18432 | tf_op jit(solution)/shard_map/all_gather | solution.py:21
  409.9 6.6 %all-gather.42.cloned.1.call-done = f32[4096,512]{1,0:T(8,128)} async-done(((f32[512,512]{1,0:T(8,128)}), f32[4096,512]{1,0:T(8,128)}) %all-gather.42.cloned.1.call-update) | async-done | bytes 8388624 | tf_op jit(solution)/shard_map/all_gather | solution.py:21
  418.9 2.5 fusion.41
  (201 shorter events, 121.5 us)
Async XLA Ops:
  7.2 354.8 %copy-start = (f32[2,128,512]{2,1,0:T(8,128)S(1)}, f32[2,128,512]{2,1,0:T(8,128)}, u32[]{:S(2)}) copy-start(f32[2,128,512]{2,1,0:T(8,128)} %param.11) | copy-start | bytes 1572868
  7.2 39.6 %all-gather.30.cloned.1.call-start = ((), (), s32[]{:S(2)}) async-start(), calls=%async_computation.1 | async-start | bytes 2621440 | tf_op jit(solution)/shard_map/all_gather | solution.py:46
  7.9 74.1 %all-gather.28.cloned.1.call-start = ((), (), s32[]{:S(2)}) async-start(), calls=%async_computation | async-start | bytes 2621440 | tf_op jit(solution)/shard_map/all_gather | solution.py:47
  8.7 92.0 %all-gather.32.cloned.1.call-start = ((), (), s32[]{:S(2)}) async-start(), calls=%async_computation.2 | async-start | bytes 3145728 | tf_op jit(solution)/shard_map/all_gather | solution.py:21
  48.5 73.3 %copy-start.6 = (f32[1,4,128,512]{3,2,0,1:T(8,128)}, f32[1,4,128,512]{3,2,0,1:T(8,128)S(1)}, u32[]{:S(2)}) copy-start(f32[1,4,128,512]{3,2,0,1:T(8,128)S(1)} %get-tuple-element.11) | copy-start | bytes 3145732
  48.5 73.3 %copy-start.8 = (f32[1,4,128,512]{3,2,0,1:T(8,128)}, f32[1,4,128,512]{3,2,0,1:T(8,128)S(1)}, u32[]{:S(2)}) copy-start(f32[1,4,128,512]{3,2,0,1:T(8,128)S(1)} %get-tuple-element.10) | copy-start | bytes 3145732
  51.4 68.2 %all-gather.38.cloned.1.call-start = ((), (), s32[]{:S(2)}) async-start(), calls=%async_computation.5 | async-start | bytes 3145728 | tf_op jit(solution)/shard_map/all_gather | solution.py:21
  86.4 86.0 %all-gather.34.cloned.1.call-start = ((), (), s32[]{:S(2)}) async-start(), calls=%async_computation.3 | async-start | bytes 5242880 | tf_op jit(solution)/shard_map/all_gather | solution.py:21
  108.0 117.2 %all-gather.40.cloned.1.call-start = ((), (), s32[]{:S(2)}) async-start(), calls=%async_computation.6 | async-start | bytes 5242880 | tf_op jit(solution)/shard_map/all_gather | solution.py:21
  122.8 65.1 %copy-start.31 = (f32[2,128,128]{2,1,0:T(8,128)S(1)}, f32[2,128,128]{2,1,0:T(8,128)}, u32[]{:S(2)}) copy-start(f32[2,128,128]{2,1,0:T(8,128)} %param.12) | copy-start | bytes 393220
  122.8 65.1 %copy-start.34 = (f32[2,128]{1,0:T(2,128)S(1)}, f32[2,128]{1,0:T(2,128)}, u32[]{:S(2)}) copy-start(f32[2,128]{1,0:T(2,128)} %param.13) | copy-start | bytes 3076
  126.9 78.1 %copy-start.3 = (f32[2,512,512]{2,1,0:T(8,128)S(1)}, f32[2,512,512]{2,1,0:T(8,128)}, u32[]{:S(2)}) copy-start(f32[2,512,512]{2,1,0:T(8,128)} %all-gather.28.cloned.1.call-done) | copy-start | bytes 6291460
  126.9 194.9 %all-gather.36.cloned.1.call-start = ((), (), s32[]{:S(2)}) async-start(), calls=%async_computation.4 | async-start | bytes 9437184 | tf_op jit(solution)/shard_map/all_gather | solution.py:21
  187.8 228.7 %all-gather.42.cloned.1.call-start = ((), (), s32[]{:S(2)}) async-start(), calls=%async_computation.7 | async-start | bytes 9437184 | tf_op jit(solution)/shard_map/all_gather | solution.py:21
  240.6 20.6 %copy-start.5 = (f32[2048,512]{1,0:T(8,128)S(1)}, f32[2048,512]{1,0:T(8,128)}, u32[]{:S(2)}) copy-start(f32[2048,512]{1,0:T(8,128)} %all-gather.34.cloned.1.call-done) | copy-start | bytes 12582916
  240.6 50.1 %copy-start.11 = (f32[512,512]{1,0:T(8,128)S(1)}, f32[512,512]{1,0:T(8,128)}, u32[]{:S(2)}) copy-start(f32[512,512]{1,0:T(8,128)} %copy-done.10) | copy-start | bytes 3145732
  240.6 50.1 %copy-start.13 = (f32[512,512]{1,0:T(8,128)S(1)}, f32[512,512]{1,0:T(8,128)}, u32[]{:S(2)}) copy-start(f32[512,512]{1,0:T(8,128)} %copy-done.12) | copy-start | bytes 3145732
  240.6 50.1 %copy-start.22 = (f32[512,512]{1,0:T(8,128)S(1)}, f32[512,512]{1,0:T(8,128)}, u32[]{:S(2)}) copy-start(f32[512,512]{1,0:T(8,128)} %fusion.129) | copy-start | bytes 3145732
  240.6 50.1 %copy-start.24 = (f32[512,512]{1,0:T(8,128)S(1)}, f32[512,512]{1,0:T(8,128)}, u32[]{:S(2)}) copy-start(f32[512,512]{1,0:T(8,128)} %copy-done.23) | copy-start | bytes 3145732
  260.0 33.8 %copy-start.17 = (f32[512,512]{1,0:T(8,128)S(1)}, f32[512,512]{1,0:T(8,128)}, u32[]{:S(2)}) copy-start(f32[512,512]{1,0:T(8,128)} %copy-done.16) | copy-start | bytes 3145732
  260.0 33.8 %copy-start.19 = (f32[512,512]{1,0:T(8,128)S(1)}, f32[512,512]{1,0:T(8,128)}, u32[]{:S(2)}) copy-start(f32[512,512]{1,0:T(8,128)} %copy-done.18) | copy-start | bytes 3145732
  260.0 33.8 %copy-start.20 = (f32[512,512]{1,0:T(8,128)S(1)}, f32[512,512]{1,0:T(8,128)}, u32[]{:S(2)}) copy-start(f32[512,512]{1,0:T(8,128)} %fusion.77) | copy-start | bytes 3145732
  260.0 33.8 %copy-start.26 = (f32[512,512]{1,0:T(8,128)S(1)}, f32[512,512]{1,0:T(8,128)}, u32[]{:S(2)}) copy-start(f32[512,512]{1,0:T(8,128)} %copy-done.25) | copy-start | bytes 3145732
  261.2 32.6 %copy-start.28 = (f32[512,512]{1,0:T(8,128)}, f32[512,512]{1,0:T(8,128)S(1)}, u32[]{:S(2)}) copy-start(f32[512,512]{1,0:T(8,128)S(1)} %fusion.15) | copy-start | bytes 3145732
  321.8 20.6 %copy-start.2 = (f32[4096,512]{1,0:T(8,128)S(1)}, f32[4096,512]{1,0:T(8,128)}, u32[]{:S(2)}) copy-start(f32[4096,512]{1,0:T(8,128)} %all-gather.36.cloned.1.call-done) | copy-start | bytes 25165828
  352.9 6.1 %copy-start.32 = (f32[512]{0:T(512)S(1)}, f32[512]{0:T(512)}, u32[]{:S(2)}) copy-start(f32[512]{0:T(512)} %param.7) | copy-start | bytes 6148
  352.9 7.1 %copy-start.9 = (f32[1,4,128,512]{3,2,0,1:T(8,128)S(1)}, f32[1,4,128,512]{3,2,0,1:T(8,128)}, u32[]{:S(2)}) copy-start(f32[1,4,128,512]{3,2,0,1:T(8,128)} %copy-done.8) | copy-start | bytes 3145732
  352.9 8.1 %copy-start.7 = (f32[1,4,128,512]{3,2,0,1:T(8,128)S(1)}, f32[1,4,128,512]{3,2,0,1:T(8,128)}, u32[]{:S(2)}) copy-start(f32[1,4,128,512]{3,2,0,1:T(8,128)} %copy-done.6) | copy-start | bytes 3145732
  354.8 20.8 %copy-start.30 = (f32[1024,512]{1,0:T(8,128)S(1)}, f32[1024,512]{1,0:T(8,128)}, u32[]{:S(2)}) copy-start(f32[1024,512]{1,0:T(8,128)} %all-gather.38.cloned.1.call-done) | copy-start | bytes 6291460
  354.8 31.3 %copy-start.4 = (f32[2048,512]{1,0:T(8,128)S(1)}, f32[2048,512]{1,0:T(8,128)}, u32[]{:S(2)}) copy-start(f32[2048,512]{1,0:T(8,128)} %all-gather.40.cloned.1.call-done) | copy-start | bytes 12582916
  357.1 51.8 %copy-start.29 = (f32[512,512]{1,0:T(8,128)S(1)}, f32[512,512]{1,0:T(8,128)}, u32[]{:S(2)}) copy-start(f32[512,512]{1,0:T(8,128)} %copy-done.28) | copy-start | bytes 3145732
  416.5 20.5 %copy-start.1 = (f32[4096,512]{1,0:T(8,128)S(1)}, f32[4096,512]{1,0:T(8,128)}, u32[]{:S(2)}) copy-start(f32[4096,512]{1,0:T(8,128)} %all-gather.42.cloned.1.call-done) | copy-start | bytes 25165828
  (11 other events, 25.9 us)
Sparse Core Ops, SparseCore 0:
  9.8 36.9 all-gather.29
  48.6 33.3 all-gather.27
  83.8 16.8 all-gather.31
  102.3 17.1 all-gather.37
  121.2 51.1 all-gather.33
  174.1 51.0 all-gather.39
  227.0 94.7 all-gather.35
  323.6 92.9 all-gather.41
